TPU v7x, 32 devices: a whole 2x2x4 slice. The times are simulated.
32 devices in a mesh: rows: 8 (over z, x), bal: 4 (over y, core).
Axes of the slice: x: 2, y: 2, z: 4, core: 2. Of those that a mesh axis runs over, the one named last changes fastest.
Arguments:
- embeddings: bfloat16 [16384, 1024], P(('rows', 'bal')), may hold values from -60 to 60
- cluster_blocks: int32 [16], replicated, may hold values from 1 to 4, as said below
Outputs:
- row_max: float32 [16384], P(('rows', 'bal'))
Inputs may be any that keep to these rules, and one draw needn't show every extreme that they name: `cluster_blocks`: the sizes sum to 32; at least one cluster has exactly 4 blocks.
All inputs are finite; a program needn't handle non-finite values.
Results may differ from a plain program's by a relative error of at most 0.00051.
Values may be sent and summed in bfloat16 or wider, within the bound.
A program may use at most 64 MiB of HBM per device.

v0:
```python
import jax
import jax.numpy as jnp
from jax import lax
from jax.sharding import PartitionSpec as P

MAXB = 4


EPSILON = 1e-06


def passed_along(block, axis, distance):
    devices = range(lax.axis_size(axis))
    route = [(i - distance, i) for i in devices if i - distance in devices]
    return lax.ppermute(block, axis, route)


def unit_rows(block_rows):
    values = block_rows.astype(jnp.float32)
    scaled = values * lax.rsqrt(jnp.sum(values * values, axis=1, keepdims=True) + EPSILON)
    return scaled.astype(jnp.bfloat16)


def joined(bounds, lower, upper):
    crossing = jnp.sum(((bounds > lower) & (bounds <= upper)).astype(jnp.int32))
    return (lower >= 0) & (crossing == 0)


def products_of(normed, partner):
    return lax.dot_general(
        normed, partner, (((1,), (1,)), ((), ())), preferred_element_type=jnp.float32
    )


def tile_maxima(normed, partner, allowed):
    products = products_of(normed, partner)
    row_part = jnp.max(products, axis=1)
    col_part = jnp.max(products, axis=0)
    return (jnp.where(allowed, row_part, -2.0), jnp.where(allowed, col_part, -2.0))


def shards(embeddings, cluster_blocks):
    normed = unit_rows(embeddings)
    bounds = jnp.cumsum(cluster_blocks)
    my_block = lax.axis_index(("rows", "bal"))
    own_products = products_of(normed, normed)
    diagonal_mask = jnp.arange(normed.shape[0])[:, None] == jnp.arange(normed.shape[0])[None, :]
    highest = jnp.max(jnp.where(diagonal_mask, -2.0, own_products), axis=1)
    for offset in range(1, MAXB):
        earlier_rows = passed_along(normed, ("rows", "bal"), offset)
        row_part, col_part = tile_maxima(
            normed, earlier_rows, joined(bounds, my_block - offset, my_block)
        )
        highest = jnp.maximum(highest, row_part)
        returned = passed_along(col_part, ("rows", "bal"), -offset)
        returned = jnp.where(joined(bounds, my_block, my_block + offset), returned, -2.0)
        highest = jnp.maximum(highest, returned)
    return highest


def solution(mesh):
    in_specs = (P(("rows", "bal"), None), P())
    out_specs = P(("rows", "bal"))
    return jax.shard_map(shards, mesh=mesh, in_specs=in_specs, out_specs=out_specs, check_vma=False)
```

profile of v0, /device:TPU:19, one launch (start us, length us, event | category | flops | bytes accessed | tf_op | source)
XLA Modules:
  0.0 71.6 jit_solution(7363943471137935380)
XLA Ops:
  0.0 0.0 copy-start
  0.0 1.6 %fusion = f32[512]{0:T(512)S(1)} fusion(bf16[512,1024]{1,0:T(8,128)(2,1)} %param.2), kind=kLoop, calls=%fused_computation.2 | loop fusion | flops 1572352 | bytes 1050624 | tf_op jit(solution)/shard_map/reduce_sum | solution.py:20
  1.6 0.0 copy-done
  1.6 0.0 copy-start.1
  1.6 0.2 fusion.1
  1.9 3.7 %collective-permute-start = (bf16[512,1024]{1,0:T(8,128)(2,1)S(1)}, bf16[512,1024]{1,0:T(8,128)(2,1)}, u32[]{:S(2)}, u32[]{:S(2)}) collective-permute-start(bf16[512,1024]{1,0:T(8,128)(2,1)S(1)} %fusion.1), channel_id=1, source_target_pairs={{0,1},{1,2},{2,3},{3,4},{4,5},{5,6},{6,7},{7,8},{8,9},{9,10},{10,1... | collective-permute-start | bytes 3145736 | tf_op jit(solution)/shard_map/ppermute | solution.py:15
  5.6 3.1 %collective-permute-start.2 = (bf16[512,1024]{1,0:T(8,128)(2,1)S(1)}, bf16[512,1024]{1,0:T(8,128)(2,1)S(1)}, u32[]{:S(2)}, u32[]{:S(2)}) collective-permute-start(bf16[512,1024]{1,0:T(8,128)(2,1)S(1)} %fusion.1), channel_id=1, source_target_pairs={{0,2},{1,3},{2,4},{3,5},{4,6},{5,7},{6,8},{7,9},{8,10},{9,11},{10,... | collective-permute-start | bytes 3145736 | tf_op jit(solution)/shard_map/ppermute | solution.py:15
  8.7 2.3 %collective-permute-start.4 = (bf16[512,1024]{1,0:T(8,128)(2,1)S(1)}, bf16[512,1024]{1,0:T(8,128)(2,1)S(1)}, u32[]{:S(2)}, u32[]{:S(2)}) collective-permute-start(bf16[512,1024]{1,0:T(8,128)(2,1)S(1)} %fusion.1), channel_id=1, source_target_pairs={{0,3},{1,4},{2,5},{3,6},{4,7},{5,8},{6,9},{7,10},{8,11},{9,12},{10... | collective-permute-start | bytes 3145736 | tf_op jit(solution)/shard_map/ppermute | solution.py:15
  11.0 0.0 copy-done.1
  11.0 0.1 copy.3
  11.1 0.7 %convert_reduce_fusion.4 = (s32[]{:T(128)}, s32[]{:T(128)}, s32[]{:T(128)}, s32[]{:T(128)}, s32[]{:T(128)}, /*index=5*/s32[]{:T(128)}) fusion(s32[16,1]{1,0:T(8,128)S(1)} %reduce-window.9, s32[]{:T(128)S(6)} %add.29, s32[]{:T(128)S(6)} %add.28, s32[]{:T(128)S(6)} %add.30, s32[]{:T(128)S(6)} %sub.10, s32[]{:T(128)S(6)} %sub.11, s32[]{:T(128)S(6)} %add.31, ...), kind=kLoop, calls=%fused_computation.11 | loop fusion | flops 410 | bytes 116 | tf_op jit(solution)/shard_map/reduce_sum | solution.py:25
  13.7 12.3 %collective-permute-done = bf16[512,1024]{1,0:T(8,128)(2,1)} collective-permute-done((bf16[512,1024]{1,0:T(8,128)(2,1)S(1)}, bf16[512,1024]{1,0:T(8,128)(2,1)}, u32[]{:S(2)}, u32[]{:S(2)}) %collective-permute-start) | collective-permute-done | bytes 1048608 | tf_op jit(solution)/shard_map/ppermute | solution.py:15
  26.0 2.0 %fusion.3 = (f32[512]{0:T(512)S(1)}, f32[512]{0:T(512)S(1)}) fusion(bf16[512,1024]{1,0:T(8,128)(2,1)S(1)} %fusion.1, bf16[512,1024]{1,0:T(8,128)(2,1)} %collective-permute-done), kind=kOutput, calls=%fused_computation.20 | convolution fusion | flops 537394176 | bytes 2101248 | tf_op jit(solution)/shard_map/dot_general | solution.py:30
  28.1 4.3 %collective-permute-start.1 = (f32[512]{0:T(512)S(1)}, f32[512]{0:T(512)S(1)}, u32[]{:S(2)}, u32[]{:S(2)}) collective-permute-start(f32[512]{0:T(512)S(1)} %broadcast_select_fusion.1), channel_id=1, source_target_pairs={{1,0},{2,1},{3,2},{4,3},{5,4},{6,5},{7,6},{8,7},{9,8},{10,9},{11,1... | collective-permute-start | bytes 6152 | tf_op jit(solution)/shard_map/ppermute | solution.py:15
  32.4 17.7 %collective-permute-done.2 = bf16[512,1024]{1,0:T(8,128)(2,1)S(1)} collective-permute-done((bf16[512,1024]{1,0:T(8,128)(2,1)S(1)}, bf16[512,1024]{1,0:T(8,128)(2,1)S(1)}, u32[]{:S(2)}, u32[]{:S(2)}) %collective-permute-start.2) | collective-permute-done | bytes 1048608 | tf_op jit(solution)/shard_map/ppermute | solution.py:15
  50.1 0.8 %fusion.4 = (f32[512]{0:T(512)S(1)}, f32[512]{0:T(512)S(1)}) fusion(bf16[512,1024]{1,0:T(8,128)(2,1)S(1)} %fusion.1, bf16[512,1024]{1,0:T(8,128)(2,1)S(1)} %collective-permute-done.2), kind=kOutput, calls=%fused_computation.21 | convolution fusion | flops 537394176 | bytes 2101248 | tf_op jit(solution)/shard_map/dot_general | solution.py:30
  51.0 2.2 %collective-permute-start.3 = (f32[512]{0:T(512)S(1)}, f32[512]{0:T(512)S(1)}, u32[]{:S(2)}, u32[]{:S(2)}) collective-permute-start(f32[512]{0:T(512)S(1)} %broadcast_select_fusion.2), channel_id=1, source_target_pairs={{2,0},{3,1},{4,2},{5,3},{6,4},{7,5},{8,6},{9,7},{10,8},{11,9},{12,... | collective-permute-start | bytes 6152 | tf_op jit(solution)/shard_map/ppermute | solution.py:15
  53.2 1.9 %collective-permute-done.4 = bf16[512,1024]{1,0:T(8,128)(2,1)S(1)} collective-permute-done((bf16[512,1024]{1,0:T(8,128)(2,1)S(1)}, bf16[512,1024]{1,0:T(8,128)(2,1)S(1)}, u32[]{:S(2)}, u32[]{:S(2)}) %collective-permute-start.4) | collective-permute-done | bytes 1048608 | tf_op jit(solution)/shard_map/ppermute | solution.py:15
  55.1 0.8 %fusion.5 = (f32[512]{0:T(512)S(1)}, f32[512]{0:T(512)S(1)}) fusion(bf16[512,1024]{1,0:T(8,128)(2,1)S(1)} %fusion.1, bf16[512,1024]{1,0:T(8,128)(2,1)S(1)} %collective-permute-done.4), kind=kOutput, calls=%fused_computation.22 | convolution fusion | flops 537394176 | bytes 2101248 | tf_op jit(solution)/shard_map/dot_general | solution.py:30
  55.9 12.4 %collective-permute-start.5 = (f32[512]{0:T(512)S(1)}, f32[512]{0:T(512)S(1)}, u32[]{:S(2)}, u32[]{:S(2)}) collective-permute-start(f32[512]{0:T(512)S(1)} %broadcast_select_fusion), channel_id=1, source_target_pairs={{3,0},{4,1},{5,2},{6,3},{7,4},{8,5},{9,6},{10,7},{11,8},{12,9},{13... | collective-permute-start | bytes 6152 | tf_op jit(solution)/shard_map/ppermute | solution.py:15
  68.3 0.8 %fusion.2 = f32[512]{0:T(512)S(1)} fusion(bf16[512,1024]{1,0:T(8,128)(2,1)S(1)} %fusion.1), kind=kOutput, calls=%fused_computation.5 | convolution fusion | flops 537656832 | bytes 1050624 | tf_op jit(solution)/shard_map/dot_general | solution.py:30
  71.0 0.0 collective-permute-done.1
  71.0 0.0 collective-permute-done.3
  71.0 0.0 collective-permute-done.5
  71.0 0.6 select_maximum_fusion
  (5 shorter events, 0.1 us)
Async XLA Ops:
  0.0 1.6 %copy-start = (bf16[512,1024]{1,0:T(8,128)(2,1)S(1)}, bf16[512,1024]{1,0:T(8,128)(2,1)}, u32[]{:S(2)}) copy-start(bf16[512,1024]{1,0:T(8,128)(2,1)} %param.2) | copy-start | bytes 3145732
  1.6 9.4 %copy-start.1 = (s32[16]{0:T(128)S(1)}, s32[16]{0:T(128)}, u32[]{:S(2)}) copy-start(s32[16]{0:T(128)} %param.3) | copy-start | bytes 196
  1.9 24.2 %collective-permute-start = (bf16[512,1024]{1,0:T(8,128)(2,1)S(1)}, bf16[512,1024]{1,0:T(8,128)(2,1)}, u32[]{:S(2)}, u32[]{:S(2)}) collective-permute-start(bf16[512,1024]{1,0:T(8,128)(2,1)S(1)} %fusion.1), channel_id=1, source_target_pairs={{0,1},{1,2},{2,3},{3,4},{4,5},{5,6},{6,7},{7,8},{8,9},{9,10},{10,1... | collective-permute-start | bytes 3145736 | tf_op jit(solution)/shard_map/ppermute | solution.py:15
  5.6 44.5 %collective-permute-start.2 = (bf16[512,1024]{1,0:T(8,128)(2,1)S(1)}, bf16[512,1024]{1,0:T(8,128)(2,1)S(1)}, u32[]{:S(2)}, u32[]{:S(2)}) collective-permute-start(bf16[512,1024]{1,0:T(8,128)(2,1)S(1)} %fusion.1), channel_id=1, source_target_pairs={{0,2},{1,3},{2,4},{3,5},{4,6},{5,7},{6,8},{7,9},{8,10},{9,11},{10,... | collective-permute-start | bytes 3145736 | tf_op jit(solution)/shard_map/ppermute | solution.py:15
  8.7 46.4 %collective-permute-start.4 = (bf16[512,1024]{1,0:T(8,128)(2,1)S(1)}, bf16[512,1024]{1,0:T(8,128)(2,1)S(1)}, u32[]{:S(2)}, u32[]{:S(2)}) collective-permute-start(bf16[512,1024]{1,0:T(8,128)(2,1)S(1)} %fusion.1), channel_id=1, source_target_pairs={{0,3},{1,4},{2,5},{3,6},{4,7},{5,8},{6,9},{7,10},{8,11},{9,12},{10... | collective-permute-start | bytes 3145736 | tf_op jit(solution)/shard_map/ppermute | solution.py:15
  28.1 42.9 %collective-permute-start.1 = (f32[512]{0:T(512)S(1)}, f32[512]{0:T(512)S(1)}, u32[]{:S(2)}, u32[]{:S(2)}) collective-permute-start(f32[512]{0:T(512)S(1)} %broadcast_select_fusion.1), channel_id=1, source_target_pairs={{1,0},{2,1},{3,2},{4,3},{5,4},{6,5},{7,6},{8,7},{9,8},{10,9},{11,1... | collective-permute-start | bytes 6152 | tf_op jit(solution)/shard_map/ppermute | solution.py:15
  51.0 20.0 %collective-permute-start.3 = (f32[512]{0:T(512)S(1)}, f32[512]{0:T(512)S(1)}, u32[]{:S(2)}, u32[]{:S(2)}) collective-permute-start(f32[512]{0:T(512)S(1)} %broadcast_select_fusion.2), channel_id=1, source_target_pairs={{2,0},{3,1},{4,2},{5,3},{6,4},{7,5},{8,6},{9,7},{10,8},{11,9},{12,... | collective-permute-start | bytes 6152 | tf_op jit(solution)/shard_map/ppermute | solution.py:15
  55.9 15.1 %collective-permute-start.5 = (f32[512]{0:T(512)S(1)}, f32[512]{0:T(512)S(1)}, u32[]{:S(2)}, u32[]{:S(2)}) collective-permute-start(f32[512]{0:T(512)S(1)} %broadcast_select_fusion), channel_id=1, source_target_pairs={{3,0},{4,1},{5,2},{6,3},{7,4},{8,5},{9,6},{10,7},{11,8},{12,9},{13... | collective-permute-start | bytes 6152 | tf_op jit(solution)/shard_map/ppermute | solution.py:15
where the time goes:
time: 71.9 us; the launch traced here: 71.6 us
  waiting for transfers between devices  32 us (45%)
  starting transfers between devices  27.9 us (39%)
  matrix products  4.45 us (6%)
  between operations  3.91 us (5%)
  other arithmetic  3.22 us (4%)
    ppermute x6, waiting for transfers between devices, passed_along(): return lax.ppermute(block, axis, route)  32 us
    ppermute x6, starting transfers between devices, passed_along(): return lax.ppermute(block, axis, route)  27.9 us
    dot_general x4, matrix products, products_of(): lax.dot_general(normed, partner, (((1,), (1,)), ((), ())), preferred_elem...  4.45 us
    reduce_sum x1, other arithmetic, unit_rows(): jnp.sum(values * values, axis=1, keepdims=True) + EPSILON  1.59 us
  transfers between devices with their start and end apart: 6, of which 3 were waited for; matrix products, arithmetic and copies ran while one was open for 7% of the time, Pallas kernels for 0%

commit v1 on v0

v1 whole, which is shorter than its diff:
```python
import functools

import jax
import jax.numpy as jnp
from jax import lax
from jax.experimental import pallas as pl
from jax.experimental.pallas import tpu as pltpu
from jax.sharding import PartitionSpec as P

EPSILON = 1e-06
LOW = -2.0
MESH_ID = pl.DeviceIdType.MESH
PIECES = 8


def nearest_kernel(sizes, counts_ref, x_ref, out_ref, raw, pair, two_back, three_back,
                   row_two, row_three, best, part_out, ret_out, ret3_out, part_in, ret_in, ret3_in,
                   load_sem, pair_send, pair_recv, two_send, two_recv, three_send, three_recv,
                   small_send, small_recv):
    n_rows, n_bal = sizes
    total = n_rows * n_bal
    block, width = x_ref.shape
    piece = block // PIECES
    me = lax.axis_index("rows") * n_bal + lax.axis_index("bal")
    odd = lax.rem(me, 2)
    quarter = lax.rem(me, 4)
    partner = me + 1 - 2 * odd
    is_even = odd == 0
    is_odd = odd == 1

    has_later = me + 2 < total
    has_earlier = me >= 2
    has_later3 = is_odd & (me + 3 < total)
    has_earlier3 = is_even & (me >= 3)
    sends_direct = has_later & ((quarter != 3) | (me + 3 >= total))
    relays = has_earlier3 & (quarter == 2)
    relayed_to = has_earlier & (quarter == 1) & (me + 1 < total)

    def coords(index):
        return (index // n_bal, lax.rem(index, n_bal))

    barrier = pltpu.get_barrier_semaphore()
    greeted = jnp.int32(0)
    for there, index in (
        (me >= 0, partner),
        (has_later, me + 2),
        (has_earlier, me - 2),
        (has_later3, me + 3),
        (has_earlier3, me - 3),
        (relays, me - 1),
        (relayed_to, me + 1),
    ):
        @pl.when(there)
        def _():
            pl.semaphore_signal(barrier, inc=1, device_id=coords(index), device_id_type=MESH_ID)
        greeted = greeted + there.astype(jnp.int32)

    load = pltpu.make_async_copy(x_ref, raw, load_sem)
    load.start()

    def count(i, carry):
        end, crossings = carry
        end = end + counts_ref[i]
        found = []
        for (lower, upper), old in zip(spans, crossings):
            found.append(old + ((end > lower) & (end <= upper)).astype(jnp.int32))
        return end, tuple(found)

    spans = ((me - 3, me), (me - 2, me), (me - 1, me), (me, me + 1), (me - 2, partner))
    zero = jnp.int32(0)
    _, crossings = lax.fori_loop(0, counts_ref.shape[0], count, (zero, (zero,) * len(spans)))
    near3 = crossings[0] == 0
    near2 = crossings[1] == 0
    near_partner = jnp.where(is_odd, crossings[2], crossings[3]) == 0
    near2_partner = crossings[4] == 0

    load.wait()

    @pl.loop(0, PIECES)
    def _(q):
        rows = pl.ds(pl.multiple_of(q * piece, piece), piece)
        values = raw[rows, :].astype(jnp.float32)
        scale = lax.rsqrt(jnp.sum(values * values, axis=1, keepdims=True) + EPSILON)
        pair[0, rows, :] = (values * scale).astype(jnp.bfloat16)

    pl.semaphore_wait(barrier, greeted)

    def rows_of(q):
        return pl.ds(pl.multiple_of(q * piece, piece), piece)

    def to_two(q):
        return pltpu.make_async_remote_copy(
            src_ref=pair.at[0, rows_of(q)], dst_ref=two_back.at[rows_of(q)],
            send_sem=two_send.at[q], recv_sem=two_recv.at[q],
            device_id=coords(me + 2), device_id_type=MESH_ID)

    def to_three(q):
        return pltpu.make_async_remote_copy(
            src_ref=pair.at[0, rows_of(q)], dst_ref=three_back.at[rows_of(q)],
            send_sem=three_send.at[q], recv_sem=three_recv.at[q],
            device_id=coords(me + 3), device_id_type=MESH_ID)

    def onward(q):
        return pltpu.make_async_remote_copy(
            src_ref=three_back.at[rows_of(q)], dst_ref=two_back.at[rows_of(q)],
            send_sem=three_send.at[q], recv_sem=two_recv.at[q],
            device_id=coords(me - 1), device_id_type=MESH_ID)

    def to_partner():
        return pltpu.make_async_remote_copy(
            src_ref=pair.at[0], dst_ref=pair.at[1],
            send_sem=pair_send, recv_sem=pair_recv,
            device_id=coords(partner), device_id_type=MESH_ID)

    def small(slot, src, dst, index):
        return pltpu.make_async_remote_copy(
            src_ref=src, dst_ref=dst, send_sem=small_send.at[slot], recv_sem=small_recv.at[slot],
            device_id=coords(index), device_id_type=MESH_ID)

    to_partner().start()

    @pl.loop(0, PIECES)
    def _(q):
        @pl.when(has_later3)
        def _():
            to_three(q).start()

        @pl.when(sends_direct)
        def _():
            to_two(q).start()

    def products(left, right):
        return lax.dot_general(left, right, (((1,), (1,)), ((), ())),
                               preferred_element_type=jnp.float32)

    step = 128
    best[...] = jnp.full(best.shape, LOW, jnp.float32)

    @pl.loop(0, block // step)
    def _(s):
        rows = pl.ds(pl.multiple_of(s * step, step), step)
        own = products(pair[0, rows, :], pair[0])
        across = lax.broadcasted_iota(jnp.int32, own.shape, 1)
        down = lax.broadcasted_iota(jnp.int32, own.shape, 0) + s * step
        own = jnp.where(across == down, LOW, own)
        best[0:1, :] = jnp.maximum(best[0:1, :], jnp.max(own, axis=0, keepdims=True))

    to_partner().wait()

    @pl.loop(0, block // step)
    def _(s):
        rows = pl.ds(pl.multiple_of(s * step, step), step)
        other = products(pair[1, rows, :], pair[0])
        top = jnp.max(other, axis=0, keepdims=True)
        best[0:1, :] = jnp.maximum(best[0:1, :], jnp.where(near_partner, top, LOW))

    def lanes_max(tile):
        highest = tile[:, :128]
        for start in range(128, tile.shape[1], 128):
            highest = jnp.maximum(highest, tile[:, start:start + 128])
        return highest

    @pl.loop(0, PIECES)
    def _(q):
        rows = rows_of(q)

        @pl.when(has_earlier3)
        def _():
            to_three(q).wait_recv()

            @pl.when(relays)
            def _():
                onward(q).start()

            tile = products(three_back[rows, :], pair[0])
            row_three[rows, :] = lanes_max(tile)
            top = jnp.max(tile, axis=0, keepdims=True)
            best[0:1, :] = jnp.maximum(best[0:1, :], jnp.where(near3, top, LOW))

        @pl.when(has_earlier)
        def _():
            to_two(q).wait_recv()
            tile = products(two_back[rows, :], pair[0])
            other = products(two_back[rows, :], pair[1])
            row_two[rows, :] = jnp.maximum(
                jnp.where(near2, lanes_max(tile), LOW),
                jnp.where(near2_partner, lanes_max(other), LOW))
            top = jnp.max(tile, axis=0, keepdims=True)
            best[0:1, :] = jnp.maximum(best[0:1, :], jnp.where(near2, top, LOW))
            top = jnp.max(other, axis=0, keepdims=True)
            best[1:2, :] = jnp.maximum(best[1:2, :], jnp.where(near2_partner, top, LOW))

    @pl.when(has_earlier)
    def _():
        ret_out[...] = jnp.max(row_two[...].T, axis=0, keepdims=True)
        part_out[...] = best[1:2, :]
        small(0, ret_out, ret_in, me - 2).start()
        small(1, part_out, part_in, partner).start()

    @pl.when(has_earlier3)
    def _():
        top = jnp.max(row_three[...].T, axis=0, keepdims=True)
        ret3_out[...] = jnp.where(near3, top, LOW)
        small(2, ret3_out, ret3_in, me - 3).start()

    @pl.when(has_earlier)
    def _():
        small(1, part_out, part_in, partner).wait()
        best[0:1, :] = jnp.maximum(best[0:1, :], part_in[...])

    @pl.when(has_later3)
    def _():
        small(2, ret3_out, ret3_in, me + 3).wait_recv()
        best[0:1, :] = jnp.maximum(best[0:1, :], ret3_in[...])

    @pl.when(has_later)
    def _():
        small(0, ret_out, ret_in, me + 2).wait_recv()
        best[0:1, :] = jnp.maximum(best[0:1, :], ret_in[...])

    out_ref[...] = best[0:1, :]

    @pl.loop(0, PIECES)
    def _(q):
        @pl.when(has_later3)
        def _():
            to_three(q).wait_send()

        @pl.when(sends_direct)
        def _():
            to_two(q).wait_send()

        @pl.when(relays)
        def _():
            onward(q).wait_send()

    @pl.when(has_earlier)
    def _():
        small(0, ret_out, ret_in, me - 2).wait_send()

    @pl.when(has_earlier3)
    def _():
        small(2, ret3_out, ret3_in, me - 3).wait_send()


def shards(sizes, embeddings, cluster_blocks):
    block, width = embeddings.shape
    line = pltpu.VMEM((1, block), jnp.float32)
    wide = pltpu.VMEM((block, width), jnp.bfloat16)
    flags = pltpu.SemaphoreType.DMA((PIECES,))
    lone = pltpu.SemaphoreType.DMA
    out = pl.pallas_call(
        functools.partial(nearest_kernel, sizes),
        out_shape=jax.ShapeDtypeStruct((1, block), jnp.float32),
        in_specs=[pl.BlockSpec(memory_space=pltpu.SMEM), pl.BlockSpec(memory_space=pl.ANY)],
        out_specs=pl.BlockSpec(memory_space=pltpu.VMEM),
        scratch_shapes=[
            wide, pltpu.VMEM((2, block, width), jnp.bfloat16), wide, wide,
            pltpu.VMEM((block, 128), jnp.float32), pltpu.VMEM((block, 128), jnp.float32),
            pltpu.VMEM((8, block), jnp.float32),
            line, line, line, line, line, line,
            lone, lone, lone, flags, flags, flags, flags,
            pltpu.SemaphoreType.DMA((3,)), pltpu.SemaphoreType.DMA((3,)),
        ],
        compiler_params=pltpu.CompilerParams(collective_id=0, has_side_effects=True),
        name="nearest",
    )(cluster_blocks, embeddings)
    return out.reshape(-1)


def solution(mesh):
    sizes = (mesh.shape["rows"], mesh.shape["bal"])
    return jax.shard_map(
        functools.partial(shards, sizes), mesh=mesh,
        in_specs=(P(("rows", "bal"), None), P()), out_specs=P(("rows", "bal")), check_vma=False)
```

time: 71.9 us -> 36.6 us (0.51)
  the two profiles are of different devices: /device:TPU:19 before, /device:TPU:7 now
where the time goes in v1:
time: 36.6 us; the launch traced here: 36.4 us
  Pallas kernels  35.1 us (96%)
  local copies, waits for them, and re-layouts  1.26 us (3%)
    pallas_call x1, Pallas kernels, shards(): pl.pallas_call(functools.partial(nearest_kernel, sizes), out_shape=jax.Sh...  35.1 us
    unnamed x1, local copies, waits for them, and re-layouts  1.26 us

profile of v1, /device:TPU:7, one launch (start us, length us, event | category | flops | bytes accessed | tf_op | source)
XLA Modules:
  0.0 36.4 jit_solution(810343264617958491)
XLA Ops:
  0.0 35.1 %nearest.1 = f32[1,512]{1,0:T(1,128)} custom-call(s32[16]{0:T(128)} %counts_ref.1, bf16[512,1024]{1,0:T(8,128)(2,1)} %x_ref.1), custom_call_target="tpu_custom_call" | custom-call | tf_op jit(solution)/shard_map/nearest/pallas_call | solution.py:252
  35.1 1.3 %copy.4 = f32[512]{0:T(512)} copy(f32[512]{0:T(512)} %bitcast.1) | data formatting | bytes 4096

commit v2 on v1

--- a/solution.py
+++ b/solution.py
@@ -13,10 +13,10 @@
 PIECES = 8
 
 
-def nearest_kernel(sizes, counts_ref, x_ref, out_ref, raw, pair, two_back, three_back,
+def nearest_kernel(sizes, counts_hbm, x_ref, out_ref, raw, pair, two_back, three_back,
                    row_two, row_three, best, part_out, ret_out, ret3_out, part_in, ret_in, ret3_in,
                    load_sem, pair_send, pair_recv, two_send, two_recv, three_send, three_recv,
-                   small_send, small_recv):
+                   small_send, small_recv, counts_ref, counts_sem):
     n_rows, n_bal = sizes
     total = n_rows * n_bal
     block, width = x_ref.shape
@@ -57,6 +57,65 @@
 
     load = pltpu.make_async_copy(x_ref, raw, load_sem)
     load.start()
+    counts_load = pltpu.make_async_copy(counts_hbm, counts_ref, counts_sem)
+    counts_load.start()
+
+    load.wait()
+
+    @pl.loop(0, PIECES)
+    def _(q):
+        rows = pl.ds(pl.multiple_of(q * piece, piece), piece)
+        values = raw[rows, :].astype(jnp.float32)
+        scale = lax.rsqrt(jnp.sum(values * values, axis=1, keepdims=True) + EPSILON)
+        pair[0, rows, :] = (values * scale).astype(jnp.bfloat16)
+
+    pl.semaphore_wait(barrier, greeted)
+
+    def rows_of(q):
+        return pl.ds(pl.multiple_of(q * piece, piece), piece)
+
+    def to_two(q):
+        return pltpu.make_async_remote_copy(
+            src_ref=pair.at[0, rows_of(q)], dst_ref=two_back.at[rows_of(q)],
+            send_sem=two_send.at[q], recv_sem=two_recv.at[q],
+            device_id=coords(me + 2), device_id_type=MESH_ID)
+
+    def to_three(q):
+        return pltpu.make_async_remote_copy(
+            src_ref=pair.at[0, rows_of(q)], dst_ref=three_back.at[rows_of(q)],
+            send_sem=three_send.at[q], recv_sem=three_recv.at[q],
+            device_id=coords(me + 3), device_id_type=MESH_ID)
+
+    def onward(q):
+        return pltpu.make_async_remote_copy(
+            src_ref=three_back.at[rows_of(q)], dst_ref=two_back.at[rows_of(q)],
+            send_sem=three_send.at[q], recv_sem=two_recv.at[q],
+            device_id=coords(me - 1), device_id_type=MESH_ID)
+
+    def to_partner():
+        return pltpu.make_async_remote_copy(
+            src_ref=pair.at[0], dst_ref=pair.at[1],
+            send_sem=pair_send, recv_sem=pair_recv,
+            device_id=coords(partner), device_id_type=MESH_ID)
+
+    def small(slot, src, dst, index):
+        return pltpu.make_async_remote_copy(
+            src_ref=src, dst_ref=dst, send_sem=small_send.at[slot], recv_sem=small_recv.at[slot],
+            device_id=coords(index), device_id_type=MESH_ID)
+
+    to_partner().start()
+
+    @pl.loop(0, PIECES)
+    def _(q):
+        @pl.when(has_later3)
+        def _():
+            to_three(q).start()
+
+        @pl.when(sends_direct)
+        def _():
+            to_two(q).start()
+
+    counts_load.wait()
 
     def count(i, carry):
         end, crossings = carry
@@ -73,61 +132,6 @@
     near2 = crossings[1] == 0
     near_partner = jnp.where(is_odd, crossings[2], crossings[3]) == 0
     near2_partner = crossings[4] == 0
-
-    load.wait()
-
-    @pl.loop(0, PIECES)
-    def _(q):
-        rows = pl.ds(pl.multiple_of(q * piece, piece), piece)
-        values = raw[rows, :].astype(jnp.float32)
-        scale = lax.rsqrt(jnp.sum(values * values, axis=1, keepdims=True) + EPSILON)
-        pair[0, rows, :] = (values * scale).astype(jnp.bfloat16)
-
-    pl.semaphore_wait(barrier, greeted)
-
-    def rows_of(q):
-        return pl.ds(pl.multiple_of(q * piece, piece), piece)
-
-    def to_two(q):
-        return pltpu.make_async_remote_copy(
-            src_ref=pair.at[0, rows_of(q)], dst_ref=two_back.at[rows_of(q)],
-            send_sem=two_send.at[q], recv_sem=two_recv.at[q],
-            device_id=coords(me + 2), device_id_type=MESH_ID)
-
-    def to_three(q):
-        return pltpu.make_async_remote_copy(
-            src_ref=pair.at[0, rows_of(q)], dst_ref=three_back.at[rows_of(q)],
-            send_sem=three_send.at[q], recv_sem=three_recv.at[q],
-            device_id=coords(me + 3), device_id_type=MESH_ID)
-
-    def onward(q):
-        return pltpu.make_async_remote_copy(
-            src_ref=three_back.at[rows_of(q)], dst_ref=two_back.at[rows_of(q)],
-            send_sem=three_send.at[q], recv_sem=two_recv.at[q],
-            device_id=coords(me - 1), device_id_type=MESH_ID)
-
-    def to_partner():
-        return pltpu.make_async_remote_copy(
-            src_ref=pair.at[0], dst_ref=pair.at[1],
-            send_sem=pair_send, recv_sem=pair_recv,
-            device_id=coords(partner), device_id_type=MESH_ID)
-
-    def small(slot, src, dst, index):
-        return pltpu.make_async_remote_copy(
-            src_ref=src, dst_ref=dst, send_sem=small_send.at[slot], recv_sem=small_recv.at[slot],
-            device_id=coords(index), device_id_type=MESH_ID)
-
-    to_partner().start()
-
-    @pl.loop(0, PIECES)
-    def _(q):
-        @pl.when(has_later3)
-        def _():
-            to_three(q).start()
-
-        @pl.when(sends_direct)
-        def _():
-            to_two(q).start()
 
     def products(left, right):
         return lax.dot_general(left, right, (((1,), (1,)), ((), ())),
@@ -251,8 +255,8 @@
     lone = pltpu.SemaphoreType.DMA
     out = pl.pallas_call(
         functools.partial(nearest_kernel, sizes),
-        out_shape=jax.ShapeDtypeStruct((1, block), jnp.float32),
-        in_specs=[pl.BlockSpec(memory_space=pltpu.SMEM), pl.BlockSpec(memory_space=pl.ANY)],
+        out_shape=pltpu.VMEM((1, block), jnp.float32),
+        in_specs=[pl.BlockSpec(memory_space=pl.ANY)] * 2,
         out_specs=pl.BlockSpec(memory_space=pltpu.VMEM),
         scratch_shapes=[
             wide, pltpu.VMEM((2, block, width), jnp.bfloat16), wide, wide,
@@ -261,6 +265,7 @@
             line, line, line, line, line, line,
             lone, lone, lone, flags, flags, flags, flags,
             pltpu.SemaphoreType.DMA((3,)), pltpu.SemaphoreType.DMA((3,)),
+            pltpu.SMEM(cluster_blocks.shape, jnp.int32), lone,
         ],
         compiler_params=pltpu.CompilerParams(collective_id=0, has_side_effects=True),
         name="nearest",

time: 36.6 us -> 34.6 us (0.945)
  Pallas kernels: 35.1 us -> 33.9 us
  local copies, waits for them, and re-layouts: 1.26 us -> 0.58 us
    pallas_call x1, Pallas kernels: 35.1 us -> 33.9 us  [shards(): pl.pallas_call(functools.partial(nearest_kernel, sizes), out_shape=pltpu....]
    unnamed x1, local copies, waits for them, and re-layouts: 1.26 us -> 0.58 us
where the time goes in v2:
time: 34.6 us; the launch traced here: 34.5 us
  Pallas kernels  33.9 us (98%)
  local copies, waits for them, and re-layouts  0.58 us (2%)
    pallas_call x1, Pallas kernels, shards(): pl.pallas_call(functools.partial(nearest_kernel, sizes), out_shape=pltpu....  33.9 us

profile of v2, /device:TPU:7, one launch (start us, length us, event | category | flops | bytes accessed | tf_op | source)
XLA Modules:
  0.0 34.5 jit_solution(2118920453579284350)
XLA Ops:
  0.0 33.9 %nearest.1 = f32[1,512]{1,0:T(1,128)S(1)} custom-call(s32[16]{0:T(128)} %counts_hbm.1, bf16[512,1024]{1,0:T(8,128)(2,1)} %x_ref.1), custom_call_target="tpu_custom_call" | custom-call | tf_op jit(solution)/shard_map/nearest/pallas_call | solution.py:256
  33.9 0.6 %copy.4 = f32[512]{0:T(512)} copy(f32[512]{0:T(512)S(1)} %bitcast.1) | data formatting | bytes 4096

commit v3 on v2

--- a/solution.py
+++ b/solution.py
@@ -55,16 +55,22 @@
             pl.semaphore_signal(barrier, inc=1, device_id=coords(index), device_id_type=MESH_ID)
         greeted = greeted + there.astype(jnp.int32)
 
-    load = pltpu.make_async_copy(x_ref, raw, load_sem)
-    load.start()
+    def load(q):
+        rows = pl.ds(pl.multiple_of(q * piece, piece), piece)
+        return pltpu.make_async_copy(x_ref.at[rows], raw.at[rows], load_sem.at[q])
+
+    @pl.loop(0, PIECES)
+    def _(q):
+        load(q).start()
+
     counts_load = pltpu.make_async_copy(counts_hbm, counts_ref, counts_sem)
     counts_load.start()
 
-    load.wait()
 
     @pl.loop(0, PIECES)
     def _(q):
         rows = pl.ds(pl.multiple_of(q * piece, piece), piece)
+        load(q).wait()
         values = raw[rows, :].astype(jnp.float32)
         scale = lax.rsqrt(jnp.sum(values * values, axis=1, keepdims=True) + EPSILON)
         pair[0, rows, :] = (values * scale).astype(jnp.bfloat16)
@@ -263,7 +269,7 @@
             pltpu.VMEM((block, 128), jnp.float32), pltpu.VMEM((block, 128), jnp.float32),
             pltpu.VMEM((8, block), jnp.float32),
             line, line, line, line, line, line,
-            lone, lone, lone, flags, flags, flags, flags,
+            flags, lone, lone, flags, flags, flags, flags,
             pltpu.SemaphoreType.DMA((3,)), pltpu.SemaphoreType.DMA((3,)),
             pltpu.SMEM(cluster_blocks.shape, jnp.int32), lone,
         ],

time: 34.6 us -> 34.4 us (level)
  no operation moved by 1% of the time
where the time goes in v3:
time: 34.4 us; the launch traced here: 34.2 us
  Pallas kernels  33.6 us (98%)
  local copies, waits for them, and re-layouts  0.58 us (2%)
    pallas_call x1, Pallas kernels, shards(): pl.pallas_call(functools.partial(nearest_kernel, sizes), out_shape=pltpu....  33.6 us

profile of v3, /device:TPU:7, one launch (start us, length us, event | category | flops | bytes accessed | tf_op | source)
XLA Modules:
  0.0 34.2 jit_solution(91923784879084338)
XLA Ops:
  0.0 33.6 %nearest.1 = f32[1,512]{1,0:T(1,128)S(1)} custom-call(s32[16]{0:T(128)} %counts_hbm.1, bf16[512,1024]{1,0:T(8,128)(2,1)} %x_ref.1), custom_call_target="tpu_custom_call" | custom-call | tf_op jit(solution)/shard_map/nearest/pallas_call | solution.py:262
  33.6 0.6 %copy.4 = f32[512]{0:T(512)} copy(f32[512]{0:T(512)S(1)} %bitcast.1) | data formatting | bytes 4096
